TPU v7x, 32 devices: a 4x2x2 block of a 4x4x8 slice. The times are simulated.
32 devices in a mesh: frag: 4 (over y, z), dev: 8 (over x, core).
Axes of the slice: x: 4, y: 2, z: 2, core: 2. Of those that a mesh axis runs over, the one named last changes fastest.
The devices are a block of a 4x4x8 slice.
Arguments:
- a_ints: bfloat16 [416, 104, 104, 104], P(('frag', 'dev')), parts along dimension 0
- c_occ: bfloat16 [416, 32], P('frag'), parts along dimension 0
- c_vir: bfloat16 [416, 64], P('frag'), parts along dimension 0
- eps_occ: float32 [128], P('frag'), parts along dimension 0
- eps_vir: float32 [256], P('frag'), parts along dimension 0
Outputs:
- output: float32 [128, 32], P('frag', 'dev'), parts along dimension 0
There are 4 independent parts. A program takes and returns all parts, laid end to end along the dimension named above; each array names one.
All inputs are finite; a program needn't handle non-finite values.
Results may differ from a plain program's by a relative error of at most 0.001.
Values are sent between devices in bfloat16 or wider.
A program may use at most 768 MiB of HBM per device.

v0:
```python
import jax
import jax.numpy as jnp
from jax import lax
from jax.sharding import PartitionSpec as P, NamedSharding


def pair_energies(v_mo, eps_j, eps_occ, eps_vir):
    v_swap = jnp.swapaxes(v_mo, 1, 2)
    denominator = (eps_j[:, None, None, None] + eps_occ[None, None, None, :]
                   - eps_vir[None, :, None, None] - eps_vir[None, None, :, None])
    pair_ji = jnp.sum(v_mo * (2.0 * v_mo - v_swap) / denominator, axis=(1, 2))
    return pair_ji.T


def solution(mesh):
    group_size = mesh.shape["dev"]

    def per_device(a_ints, c_occ, c_vir, eps_occ, eps_vir):
        occ_dev = c_occ.shape[1] // group_size
        t_one = jnp.einsum("pqrs,rj->pqsj", a_ints, c_occ, preferred_element_type=jnp.float32).astype(jnp.bfloat16)
        half_mo = jnp.einsum("pqsj,sb->pqjb", t_one, c_vir, preferred_element_type=jnp.float32).astype(jnp.bfloat16)
        half_mo = lax.all_to_all(half_mo, "dev", 2, 0, tiled=True)
        g_mat = jnp.einsum("pqjb,qa->pjba", half_mo, c_vir, preferred_element_type=jnp.float32).astype(jnp.bfloat16)
        v_mo = jnp.einsum("pjba,pi->jbai", g_mat, c_occ, preferred_element_type=jnp.float32)
        eps_j = lax.dynamic_slice_in_dim(eps_occ, lax.axis_index("dev") * occ_dev, occ_dev)
        return pair_energies(v_mo, eps_j, eps_occ, eps_vir)

    return jax.shard_map(
        per_device,
        mesh=mesh,
        in_specs=(P(("frag", "dev")), P("frag"), P("frag"), P("frag"), P("frag")),
        out_specs=P("frag", "dev"),
        check_vma=False,
    )
```

profile of v0, /device:TPU:81, one launch (start us, length us, event | category | flops | bytes accessed | tf_op | source)
XLA Modules:
  0.0 156.8 jit_solution(17759605580530101393)
XLA Ops:
  0.0 0.0 copy-start
  0.0 13.2 %convolution_convert_fusion = bf16[13,104,104,32]{2,3,1,0:T(8,128)(2,1)S(1)} fusion(bf16[13,104,104,104]{3,2,1,0:T(8,128)(2,1)} %param.5, bf16[104,32]{0,1:T(8,128)(2,1)} %param.6), kind=kOutput, calls=%fused_computation.5 | convolution fusion | flops 940386304 | bytes 38252032 | tf_op jit(solution)/shard_map/pqrs,rj->pqsj/dot_general | solution.py:20
  13.2 0.0 copy-done
  13.3 15.1 %fusion.2 = bf16[13,104,32,64]{1,3,2,0:T(8,128)(2,1)} fusion(bf16[13,104,104,32]{2,3,1,0:T(8,128)(2,1)S(1)} %convolution_convert_fusion, bf16[104,64]{0,1:T(8,128)(2,1)S(1)} %copy-done), kind=kOutput, calls=%fused_computation.2 | convolution fusion | flops 578699264 | bytes 14550016 | tf_op jit(solution)/shard_map/pqsj,sb->pqjb/dot_general | solution.py:21
  28.3 7.5 %copy.14 = bf16[13,104,32,64]{1,3,0,2:T(8,128)(2,1)} copy(bf16[13,104,32,64]{1,3,2,0:T(8,128)(2,1)} %fusion.2) | data formatting | bytes 11075584 | tf_op jit(solution)/shard_map/convert_element_type | solution.py:21
  35.8 0.0 copy-start.3
  35.8 0.0 copy-start.2
  35.8 6.8 %all-to-all-start = ((bf16[13,104,32,64]{1,3,0,2:T(8,128)(2,1)}), bf16[13,104,32,64]{1,3,0,2:T(8,128)(2,1)}, u32[]{:S(2)}, u32[]{:S(2)}) async-start(bf16[13,104,32,64]{1,3,0,2:T(8,128)(2,1)} %copy.14), calls=%async_computation | async-start | bytes 13631488 | tf_op jit(solution)/shard_map/all_to_all | solution.py:22
  42.7 0.0 copy-done.3
  42.7 0.1 dynamic_slice.3
  42.8 0.1 broadcast_add_fusion
  42.8 0.0 copy-done.2
  42.8 0.1 broadcast_subtract_fusion
  42.9 76.5 %all-to-all-done = bf16[13,104,32,64]{1,3,0,2:T(8,128)(2,1)} async-done(((bf16[13,104,32,64]{1,3,0,2:T(8,128)(2,1)}), bf16[13,104,32,64]{1,3,0,2:T(8,128)(2,1)}, u32[]{:S(2)}, u32[]{:S(2)}) %all-to-all-start) | async-done | bytes 5537824 | tf_op jit(solution)/shard_map/all_to_all | solution.py:22
  119.4 0.0 copy-start.1
  119.4 8.2 %copy.16 = bf16[8,13,104,4,64]{2,4,3,1,0:T(8,128)(2,1)} copy(bf16[8,13,104,4,64]{2,4,1,3,0:T(8,128)(2,1)} %bitcast.6) | data formatting | bytes 11075584 | tf_op jit(solution)/shard_map/all_to_all | solution.py:22
  127.6 0.0 copy-done.1
  127.6 17.7 %fusion.9 = f32[4,64,64,32]{2,3,1,0:T(8,128)} fusion(bf16[104,104,4,64]{1,3,2,0:T(8,128)(2,1)} %bitcast.29, bf16[104,64]{0,1:T(8,128)(2,1)S(1)} %copy-done, bf16[104,32]{0,1:T(8,128)(2,1)S(1)} %copy-done.1), kind=kOutput, calls=%fused_computation.9 | convolution fusion | flops 465174528 | bytes 7654912 | tf_op jit(solution)/shard_map/pjba,pi->jbai/dot_general | solution.py:24
  145.3 6.8 %copy.18 = f32[4,64,64,32]{1,3,2,0:T(8,128)} copy(f32[4,64,64,32]{2,3,1,0:T(8,128)} %fusion.9) | data formatting | bytes 4194304 | tf_op jit(solution)/shard_map/pjba,pi->jbai/dot_general | solution.py:24
  152.1 4.8 %fusion.11 = f32[4,32]{1,0:T(4,128)} fusion(f32[4,64,64,32]{2,3,1,0:T(8,128)} %fusion.9, f32[4,64,64,32]{1,3,2,0:T(8,128)} %copy.18, f32[64]{0:T(128)S(1)} %copy-done.2, f32[4,64,32]{2,1,0:T(8,128)S(1)} %broadcast_subtract_fusion), kind=kLoop, calls=%fused_computation.11 | loop fusion | flops 3145600 | bytes 4227840 | tf_op jit(solution)/shard_map/reduce_sum | solution.py:11
Async XLA Ops:
  0.0 13.3 %copy-start = (bf16[104,64]{0,1:T(8,128)(2,1)S(1)}, bf16[104,64]{0,1:T(8,128)(2,1)}, u32[]{:S(2)}) copy-start(bf16[104,64]{0,1:T(8,128)(2,1)} %param.7) | copy-start | bytes 39940
  35.8 6.9 %copy-start.3 = (f32[32]{0:T(128)S(1)}, f32[32]{0:T(128)}, u32[]{:S(2)}) copy-start(f32[32]{0:T(128)} %param.8) | copy-start | bytes 388
  35.8 7.0 %copy-start.2 = (f32[64]{0:T(128)S(1)}, f32[64]{0:T(128)}, u32[]{:S(2)}) copy-start(f32[64]{0:T(128)} %param.9) | copy-start | bytes 772
  35.8 83.6 %all-to-all-start = ((bf16[13,104,32,64]{1,3,0,2:T(8,128)(2,1)}), bf16[13,104,32,64]{1,3,0,2:T(8,128)(2,1)}, u32[]{:S(2)}, u32[]{:S(2)}) async-start(bf16[13,104,32,64]{1,3,0,2:T(8,128)(2,1)} %copy.14), calls=%async_computation | async-start | bytes 13631488 | tf_op jit(solution)/shard_map/all_to_all | solution.py:22
  119.4 8.2 %copy-start.1 = (bf16[104,32]{0,1:T(8,128)(2,1)S(1)}, bf16[104,32]{0,1:T(8,128)(2,1)}, u32[]{:S(2)}) copy-start(bf16[104,32]{0,1:T(8,128)(2,1)} %param.6) | copy-start | bytes 19972
where the time goes:
time: 157 us
  waiting for transfers between devices  76.5 us (49%)
  matrix products  46 us (29%)
  local copies, waits for them, and re-layouts  22.6 us (14%)
  starting transfers between devices  6.85 us (4%)
  other arithmetic  4.9 us (3%)
    all_to_all x1, waiting for transfers between devices, per_device(): half_mo = lax.all_to_all(half_mo, 'dev', 2, 0, tiled=True)  76.5 us
    dot_general x1, matrix products, per_device(): jnp.einsum('pjba,pi->jbai', g_mat, c_occ, preferred_element_type=jnp.floa...  17.7 us
    dot_general x1, matrix products, per_device(): jnp.einsum('pqsj,sb->pqjb', t_one, c_vir, preferred_element_type=jnp.floa...  15.1 us
    dot_general x1, matrix products, per_device(): jnp.einsum('pqrs,rj->pqsj', a_ints, c_occ, preferred_element_type=jnp.flo...  13.2 us
    all_to_all x1, local copies, waits for them, and re-layouts, per_device(): half_mo = lax.all_to_all(half_mo, 'dev', 2, 0, tiled=True)  8.2 us
    convert_element_type x1, local copies, waits for them, and re-layouts, per_device(): jnp.einsum('pqsj,sb->pqjb', t_one, c_vir, preferred_element_type=jnp.floa...  7.48 us
    all_to_all x1, starting transfers between devices, per_device(): half_mo = lax.all_to_all(half_mo, 'dev', 2, 0, tiled=True)  6.85 us
    dot_general x1, local copies, waits for them, and re-layouts, per_device(): jnp.einsum('pjba,pi->jbai', g_mat, c_occ, preferred_element_type=jnp.floa...  6.78 us
  transfers between devices with their start and end apart: 1, of which 1 were waited for; matrix products, arithmetic and copies ran while one was open for 0% of the time, Pallas kernels for 0%

commit v1 on v0

v1 whole, which is shorter than its diff:
```python
import functools

import jax
import jax.numpy as jnp
from jax import lax
from jax.experimental import pallas as pl
from jax.experimental.pallas import tpu as pltpu
from jax.sharding import PartitionSpec as P

MESH = pl.DeviceIdType.MESH
LANES = 128
SUB = 16
F32, BF16 = jnp.float32, jnp.bfloat16


def dot(lhs, rhs):
    return jnp.dot(lhs, rhs, preferred_element_type=F32)


def groups_of(ends):
    starts = [0] + [e + 1 for e in ends[:-1]]
    return [(s, e - s + 1) for s, e in zip(starts, ends)]


def kernel(dims, a_hbm, cot_hbm, cvt_hbm, eo_hbm, ev_hbm, out_ref, abuf, cot, cvt, eo, ev, wv, tbuf, gsend, grecv, kron, vbuf, wbuf, ebuf,
           a_sem, c_sem, send_sem, recv_sem):
    rows, n, o, v, size, slots, units, groups = dims
    me, frag = lax.axis_index("dev"), lax.axis_index("frag")
    chips = size // 2
    chip, core = me // 2, me % 2
    pair = 2 * v
    od = o // size

    def peer(dx, dc):
        return lax.rem(chip + dx, chips) * 2 + lax.rem(core + dc, 2)

    relations = [(dx, dc) for dx in sorted(range(chips), key=lambda d: -min(d, chips - d)) for dc in range(2) if (dx, dc) != (0, 0)]

    barrier = pltpu.get_barrier_semaphore()
    for dx, dc in relations:
        pl.semaphore_signal(barrier, inc=1, device_id=(frag, peer(dx, dc)), device_id_type=MESH)

    small = [pltpu.make_async_copy(src, dst, c_sem.at[k]) for k, (src, dst) in enumerate([(cot_hbm, cot), (cvt_hbm, cvt), (eo_hbm, eo), (ev_hbm, ev)])]
    for copy in small:
        copy.start()

    def load(p):
        slot = lax.rem(p, slots)
        return pltpu.make_async_copy(a_hbm.at[p], abuf.at[slot], a_sem.at[slot])

    for p in range(min(slots, rows)):
        load(p).start()
    for copy in small:
        copy.wait()

    cv = jnp.pad(cvt[...].astype(F32), ((0, 0), (0, LANES - n))).T.astype(BF16)
    zero = jnp.zeros_like(cv)
    wv[...] = jnp.concatenate([jnp.concatenate([cv, zero], 1), jnp.concatenate([zero, cv], 1)], 0)

    def share(unit, group, rel):
        start, count = groups[unit][group]
        target = peer(*relations[rel])
        return pltpu.make_async_remote_copy(
            src_ref=gsend.at[target, unit, pl.ds(start, count)],
            dst_ref=grecv.at[unit, pl.ds(me * rows + start, count)],
            send_sem=send_sem.at[unit, group, rel],
            recv_sem=recv_sem.at[unit, group, rel],
            device_id=(frag, target),
            device_id_type=MESH,
        )

    def first_half(p, carry):
        slot = lax.rem(p, slots)
        load(p).wait()
        lhs = cot[...]
        fill = jnp.zeros((n, LANES - n), BF16)
        for q in range(0, n, 2):
            rhs = jnp.concatenate([abuf[slot, q], fill, abuf[slot, q + 1], fill], 1)
            t = dot(lhs, rhs)
            tbuf[pl.ds(q, o, stride=n), :] = t[:, :LANES]
            tbuf[pl.ds(q + 1, o, stride=n), :] = t[:, LANES:]

        @pl.when(p + slots < rows)
        def _():
            load(p + slots).start()

        weights = wv[...]
        for d in range(size):
            halves = []
            for u in range(units):
                j = d * od + 2 * u
                t2 = jnp.concatenate([tbuf[j * n:(j + 1) * n, :], tbuf[(j + 1) * n:(j + 2) * n, :]], 1).astype(BF16)
                halves.append(dot(t2, weights).astype(BF16))
            g = dot(cvt[...], jnp.concatenate(halves, 1)).astype(BF16)
            for u in range(units):
                gsend[d, u, p] = g[:, u * pair:(u + 1) * pair]

        for group, (start, count) in enumerate(groups[0]):
            @pl.when(p == start + count - 1)
            def _(group=group):
                if group == 0:
                    pl.semaphore_wait(barrier, len(relations))
                for rel in range(len(relations)):
                    share(0, group, rel).start()
        return carry

    lax.fori_loop(0, rows, first_half, 0)
    for unit in range(1, units):
        for group in range(len(groups[unit])):
            for rel in range(len(relations)):
                share(unit, group, rel).start()

    total = size * rows
    spread_i = (lax.broadcasted_iota(jnp.int32, (o * SUB, o), 0) // SUB == lax.broadcasted_iota(jnp.int32, (o * SUB, o), 1)).astype(F32).astype(BF16)
    by_p = dot(spread_i, cot[...]).astype(BF16)
    step = LANES * 2
    for start in range(0, total * SUB, step):
        width = min(step, total * SUB - start)
        spread_p = (lax.broadcasted_iota(jnp.int32, (total, width), 0)
                    == (lax.broadcasted_iota(jnp.int32, (total, width), 1) + start) // SUB).astype(F32).astype(BF16)
        same = (lax.broadcasted_iota(jnp.int32, (o * SUB, width), 0) % SUB == lax.broadcasted_iota(jnp.int32, (o * SUB, width), 1) % SUB)
        kron[:, start:start + width] = jnp.where(same, dot(by_p, spread_p), 0.0).astype(BF16)

    own = pl.ds(me * rows, rows)
    for unit in range(units):
        grecv[unit, own] = gsend[me, unit]

    ev_row, eo_row = ev[...], eo[...]
    diag = lax.broadcasted_iota(jnp.int32, (v, v), 0) == lax.broadcasted_iota(jnp.int32, (v, v), 1)
    ev_col = jnp.sum(jnp.where(diag, jnp.broadcast_to(ev_row, (v, v)), 0.0), 1, keepdims=True)
    at = lax.broadcasted_iota(jnp.int32, (1, o), 1)
    diag_o = lax.broadcasted_iota(jnp.int32, (o, o), 0) == lax.broadcasted_iota(jnp.int32, (o, o), 1)
    eo_col = jnp.sum(jnp.where(diag_o, jnp.broadcast_to(eo_row, (o, o)), 0.0), 1, keepdims=True)
    left = lax.broadcasted_iota(jnp.int32, (v, pair), 1) < v

    def energies(unit):
        energy_j = [jnp.sum(jnp.where(at == me * od + 2 * unit + h, eo_row, 0.0), 1, keepdims=True) for h in range(2)]
        base = jnp.concatenate([e - ev_row for e in energy_j], 1) - ev_col
        for i in range(o):
            wbuf[i] = 1.0 / (eo_col[i:i + 1, :] + base)

        for group in range(len(groups[unit])):
            for rel in range(len(relations)):
                share(unit, group, rel).wait_recv()

        for block in range(0, v, 2 * SUB):
            rhs = jnp.concatenate([grecv[unit, :, block + k * SUB:block + (k + 1) * SUB, :].reshape(total * SUB, pair) for k in range(2)], 1)
            part = dot(kron[...], rhs)
            for k in range(2):
                vbuf[:, block + k * SUB:block + (k + 1) * SUB, :] = part[:, k * pair:(k + 1) * pair].reshape(o, SUB, pair)

        for i in range(0, o, 2):
            x = vbuf[i:i + 2].reshape(2 * v, pair)
            xt = x.T
            turned = pltpu.roll(xt, v, 1)
            top = jnp.where(left, xt[:v], turned[v:])
            bottom = jnp.where(left, turned[:v], xt[v:])
            for k, swap in enumerate((top, bottom)):
                own_v = x[k * v:(k + 1) * v]
                ebuf[i + k:i + k + 1, :] = jnp.sum(own_v * (2.0 * own_v - swap) * wbuf[i + k], 0, keepdims=True)
        sums = ebuf[...]
        return [jnp.sum(sums[:, h * v:(h + 1) * v], 1, keepdims=True) for h in range(2)]

    columns = []
    for unit in range(units):
        columns += energies(unit)
    out_ref[...] = jnp.concatenate(columns, 1)

    for unit in range(units):
        for group in range(len(groups[unit])):
            for rel in range(len(relations)):
                share(unit, group, rel).wait_send()


def solution(mesh):
    size = mesh.shape["dev"]

    def per_device(a_ints, c_occ, c_vir, eps_occ, eps_vir):
        rows, n = a_ints.shape[0], a_ints.shape[1]
        o, v = c_occ.shape[1], c_vir.shape[1]
        units = o // size // 2
        slots = 4
        early = [e for e in (0, 2, 4, 8) if e < rows - 1] + [rows - 1]
        groups = [groups_of(early)] + [[(0, rows)]] * (units - 1)
        most = max(len(g) for g in groups)
        dims = (rows, n, o, v, size, slots, units, groups)
        any_spec = pl.BlockSpec(memory_space=pl.ANY)
        return pl.pallas_call(
            functools.partial(kernel, dims),
            out_shape=jax.ShapeDtypeStruct((o, o // size), F32),
            in_specs=[any_spec] * 5,
            out_specs=pl.BlockSpec(memory_space=pltpu.VMEM),
            scratch_shapes=[
                pltpu.VMEM((slots, n, n, n), BF16),
                pltpu.VMEM((o, n), BF16),
                pltpu.VMEM((v, n), BF16),
                pltpu.VMEM((1, o), F32),
                pltpu.VMEM((1, v), F32),
                pltpu.VMEM((2 * LANES, 2 * v), BF16),
                pltpu.VMEM((o * n, LANES), F32),
                pltpu.VMEM((size, units, rows, v, 2 * v), BF16),
                pltpu.VMEM((units, size * rows, v, 2 * v), BF16),
                pltpu.VMEM((o * SUB, size * rows * SUB), BF16),
                pltpu.VMEM((o, v, 2 * v), F32),
                pltpu.VMEM((o, v, 2 * v), F32),
                pltpu.VMEM((o, 2 * v), F32),
                pltpu.SemaphoreType.DMA((slots,)),
                pltpu.SemaphoreType.DMA((4,)),
                pltpu.SemaphoreType.DMA((units, most, size - 1)),
                pltpu.SemaphoreType.DMA((units, most, size - 1)),
            ],
            compiler_params=pltpu.CompilerParams(collective_id=0, has_side_effects=True, vmem_limit_bytes=62 * 2**20),
        )(a_ints, c_occ.T, c_vir.T, eps_occ.reshape(1, o), eps_vir.reshape(1, v))

    return jax.shard_map(
        per_device,
        mesh=mesh,
        in_specs=(P(("frag", "dev")), P("frag"), P("frag"), P("frag"), P("frag")),
        out_specs=P("frag", "dev"),
        check_vma=False,
    )
```

time: 157 us -> 64.1 us (0.41)
  waiting for transfers between devices: 76.5 us -> 0 us
  Pallas kernels: 0 us -> 62.5 us
  matrix products: 46 us -> 0 us
  local copies, waits for them, and re-layouts: 22.6 us -> 1.37 us
  starting transfers between devices: 6.85 us -> 0 us
  other arithmetic: 4.9 us -> 0 us
    all_to_all x1 -> x0, waiting for transfers between devices: 76.5 us -> none  [per_device(): half_mo = lax.all_to_all(half_mo, 'dev', 2, 0, tiled=True)]
    pallas_call x0 -> x1, Pallas kernels: none -> 62.5 us  [per_device(): pl.pallas_call(functools.partial(kernel, dims), out_shape=jax.ShapeDtypeS...]
    dot_general x3 -> x0, matrix products: 46 us -> none  [the longest x1 17.7 us: per_device(): jnp.einsum('pjba,pi->jbai', g_mat, c_occ, preferred_element_type=jnp.floa...]
    all_to_all x1 -> x0, local copies, waits for them, and re-layouts: 8.2 us -> none  [per_device(): half_mo = lax.all_to_all(half_mo, 'dev', 2, 0, tiled=True)]
    convert_element_type x1 -> x0, local copies, waits for them, and re-layouts: 7.48 us -> none  [per_device(): jnp.einsum('pqsj,sb->pqjb', t_one, c_vir, preferred_element_type=jnp.floa...]
    all_to_all x1 -> x0, starting transfers between devices: 6.85 us -> none  [per_device(): half_mo = lax.all_to_all(half_mo, 'dev', 2, 0, tiled=True)]
    dot_general x1 -> x0, local copies, waits for them, and re-layouts: 6.78 us -> none  [per_device(): jnp.einsum('pjba,pi->jbai', g_mat, c_occ, preferred_element_type=jnp.floa...]
    reduce_sum x1 -> x0, other arithmetic: 4.75 us -> none  [pair_energies(): pair_ji = jnp.sum(v_mo * (2.0 * v_mo - v_swap) / denominator, axis=(1, 2))]
  transfers between devices with their start and end apart: 1 -> 0, of which waited for: 1 -> 0; matrix products, arithmetic and copies ran while one was open for 0% -> 0% of each run, Pallas kernels for 0% -> 0%
where the time goes in v1:
time: 64.1 us; the launch traced here: 63.8 us
  Pallas kernels  62.5 us (98%)
  local copies, waits for them, and re-layouts  1.37 us (2%)
    pallas_call x1, Pallas kernels, per_device(): pl.pallas_call(functools.partial(kernel, dims), out_shape=jax.ShapeDtypeS...  62.5 us
    pallas_call x1, local copies, waits for them, and re-layouts, per_device(): pl.pallas_call(functools.partial(kernel, dims), out_shape=jax.ShapeDtypeS...  1.37 us

profile of v1, /device:TPU:81, one launch (start us, length us, event | category | flops | bytes accessed | tf_op | source)
XLA Modules:
  0.0 63.8 jit_solution(7165446714360836402)
XLA Ops:
  0.0 62.5 %shard_map.55 = f32[32,4]{1,0:T(8,128)} custom-call(bf16[13,104,104,104]{3,2,1,0:T(8,128)(2,1)} %a_hbm.1, bf16[32,104]{1,0:T(8,128)(2,1)} %bitcast.5, bf16[64,104]{1,0:T(8,128)(2,1)} %bitcast.4, f32[1,32]{1,0:T(1,128)} %bitcast.6, f32[1,64]{1,0:T(1,128)} %bitcast.7), custom_call_target="tpu_custom_call" | custom-call | tf_op jit(solution)/shard_map/pallas_call | solution.py:188
  62.5 1.4 %copy.6 = f32[32,4]{0,1:T(4,128)} copy(f32[32,4]{1,0:T(8,128)} %shard_map.55) | data formatting | bytes 1024 | tf_op jit(solution)/shard_map/pallas_call | solution.py:188

commit v2 on v0

v2 whole, which is shorter than its diff:
```python
import functools

import jax
import jax.numpy as jnp
from jax import lax
from jax.experimental import pallas as pl
from jax.experimental.pallas import tpu as pltpu
from jax.sharding import PartitionSpec as P

MESH = pl.DeviceIdType.MESH
LANES = 128
SUB = 16
F32, BF16 = jnp.float32, jnp.bfloat16


def dot(lhs, rhs):
    return jnp.dot(lhs, rhs, preferred_element_type=F32)


def on(condition, action):
    if isinstance(condition, bool):
        if condition:
            action()
    else:
        pl.when(condition)(action)


def kernel(dims, a_hbm, cot_hbm, cvt_hbm, eo_hbm, ev_hbm, out_ref, abuf, cot, cvt, eo, ev, lhs, wv, tbuf, hbuf, gsend, grecv, kron, vbuf, wbuf, ebuf,
           a_sem, first_sem, c_sem, send_sem, recv_sem):
    rows, n, o, v, size, slots, units, groups, parts = dims
    me, frag = lax.axis_index("dev"), lax.axis_index("frag")
    chips = size // 2
    chip, core = me // 2, me % 2
    pair = 2 * v
    od = o // size
    total = size * rows
    starts = [sum(groups[:g]) for g in range(len(groups))]

    def peer(dx, dc):
        return lax.rem(chip + dx, chips) * 2 + lax.rem(core + dc, 2)

    relations = [(dx, dc) for dx in sorted(range(chips), key=lambda d: -min(d, chips - d)) for dc in range(2) if (dx, dc) != (0, 0)]

    def load(p):
        slot = lax.rem(p, slots)
        return pltpu.make_async_copy(a_hbm.at[p], abuf.at[slot], a_sem.at[slot])

    small = [pltpu.make_async_copy(src, dst, c_sem.at[k]) for k, (src, dst) in enumerate([(cot_hbm, cot), (cvt_hbm, cvt), (eo_hbm, eo), (ev_hbm, ev)])]
    cuts = [n * k // parts // 2 * 2 for k in range(parts)] + [n]
    opening = [pltpu.make_async_copy(a_hbm.at[0, pl.ds(x, y - x)], abuf.at[0, pl.ds(x, y - x)], first_sem.at[k])
               for k, (x, y) in enumerate(zip(cuts, cuts[1:]))]
    small[0].start()
    opening[0].start()
    small[1].start()
    for copy in opening[1:]:
        copy.start()
    for p in range(1, min(slots, rows)):
        load(p).start()
    small[2].start()
    small[3].start()
    barrier = pltpu.get_barrier_semaphore()
    for dx, dc in relations:
        pl.semaphore_signal(barrier, inc=1, device_id=(frag, peer(dx, dc)), device_id_type=MESH)

    with jax.named_scope("waitC"):
        small[0].wait()
    row, col = lax.broadcasted_iota(jnp.int32, (o, o), 0), lax.broadcasted_iota(jnp.int32, (o, o), 1)
    order = (col == 2 * lax.rem(row, o // 2) + row // (o // 2)).astype(F32).astype(BF16)
    lhs[...] = dot(order, cot[...]).astype(BF16)
    def share(unit, group, rel):
        start, count = starts[group], groups[group]
        target = peer(*relations[rel])
        return pltpu.make_async_remote_copy(
            src_ref=gsend.at[target, unit, pl.ds(start, count)],
            dst_ref=grecv.at[unit, pl.ds(size * start + me * count, count)],
            send_sem=send_sem.at[unit, group, rel],
            recv_sem=recv_sem.at[unit, group, rel],
            device_id=(frag, target),
            device_id_type=MESH,
        )

    def occupied(slot, first, last):
        fill = jnp.zeros((n, LANES - n), BF16)
        for q in range(first, last, 2):
            rhs = jnp.concatenate([abuf[slot, q], fill, abuf[slot, q + 1], fill], 1)
            t = dot(lhs[...], rhs)
            tbuf[pl.ds(q, o, stride=n), :] = t[:, :LANES]
            tbuf[pl.ds(q + 1, o, stride=n), :] = t[:, LANES:]

    def first_half(p, carry):
        slot = lax.rem(p, slots)
        if isinstance(p, int):
            for k, copy in enumerate(opening):
                with jax.named_scope("waitA"):
                    copy.wait()
                if k == parts - 1:
                    small[1].wait()
                    cv = jnp.pad(cvt[...].astype(F32), ((0, 0), (0, LANES - n))).T.astype(BF16)
                    zero = jnp.zeros_like(cv)
                    wv[...] = jnp.concatenate([jnp.concatenate([cv, zero], 1), jnp.concatenate([zero, cv], 1)], 0)
                with jax.named_scope("step1"):
                    occupied(0, cuts[k], cuts[k + 1])
        else:
            with jax.named_scope("waitA"):
                load(p).wait()
            with jax.named_scope("step1"):
                occupied(slot, 0, n)

        def refill():
            load(p + slots).start()

        on(p + slots < rows, refill)

        half = o // 2 * n
        with jax.named_scope("step2"):
            hbuf[...] = dot(jnp.concatenate([tbuf[:half, :], tbuf[half:, :]], 1).astype(BF16), wv[...])
        with jax.named_scope("step3"):
            for d in range(size):
                at = [d * units + u for u in range(units)]
                h = jnp.concatenate([hbuf[k * n:(k + 1) * n, :] for k in at], 1).astype(BF16)
                g = dot(cvt[...], h).astype(BF16)
                for u in range(units):
                    gsend[d, u, p] = g[:, u * pair:(u + 1) * pair]

        for group, (start, count) in enumerate(zip(starts, groups)):
            def send(group=group):
                if group == 0:
                    with jax.named_scope("waitB"):
                        pl.semaphore_wait(barrier, len(relations))
                for unit in range(1 if group == 0 else units):
                    for rel in range(len(relations)):
                        share(unit, group, rel).start()

            on(p == start + count - 1, send)
        return carry

    first_half(0, 0)
    lax.fori_loop(1, rows, first_half, 0)
    for unit in range(1, units):
        for rel in range(len(relations)):
            share(unit, 0, rel).start()

    small[2].wait()
    small[3].wait()
    with jax.named_scope("kron"):
        spread_i = (lax.broadcasted_iota(jnp.int32, (o * SUB, o), 0) // SUB == lax.broadcasted_iota(jnp.int32, (o * SUB, o), 1)).astype(F32).astype(BF16)
        by_p = dot(spread_i, cot[...]).astype(BF16)
        for start, count in zip(starts, groups):
            for at in range(size * start * SUB, size * (start + count) * SUB, 2 * LANES):
                width = min(2 * LANES, size * (start + count) * SUB - at)
                place = (lax.broadcasted_iota(jnp.int32, (total, width), 1) + at) // SUB - size * start
                spread_p = (lax.broadcasted_iota(jnp.int32, (total, width), 0) == place // count * rows + start + place % count).astype(F32).astype(BF16)
                same = (lax.broadcasted_iota(jnp.int32, (o * SUB, width), 0) % SUB == lax.broadcasted_iota(jnp.int32, (o * SUB, width), 1) % SUB)
                kron[:, at:at + width] = jnp.where(same, dot(by_p, spread_p), 0.0).astype(BF16)

    for unit in range(units):
        for start, count in zip(starts, groups):
            grecv[unit, pl.ds(size * start + me * count, count)] = gsend[me, unit, start:start + count]

    ev_row, eo_row = ev[...], eo[...]
    diag = lax.broadcasted_iota(jnp.int32, (v, v), 0) == lax.broadcasted_iota(jnp.int32, (v, v), 1)
    ev_col = jnp.sum(jnp.where(diag, jnp.broadcast_to(ev_row, (v, v)), 0.0), 1, keepdims=True)
    eo_col = jnp.sum(jnp.where(row == col, jnp.broadcast_to(eo_row, (o, o)), 0.0), 1, keepdims=True)
    left = lax.broadcasted_iota(jnp.int32, (v, pair), 1) < v

    def integrals(unit, first, last, add):
        width = (last - first) * SUB
        for block in range(0, v, 2 * SUB):
            rhs = jnp.concatenate([grecv[unit, first:last, block + k * SUB:block + (k + 1) * SUB, :].reshape(width, pair) for k in range(2)], 1)
            part = dot(kron[:, first * SUB:last * SUB], rhs)
            for k in range(2):
                at = slice(block + k * SUB, block + (k + 1) * SUB)
                new = part[:, k * pair:(k + 1) * pair].reshape(o, SUB, pair)
                vbuf[:, at, :] = vbuf[:, at, :] + new if add else new

    def energies(unit):
        with jax.named_scope("W"):
            energy_j = [jnp.sum(jnp.where(lax.broadcasted_iota(jnp.int32, (1, o), 1) == me * od + 2 * unit + h, eo_row, 0.0), 1, keepdims=True) for h in range(2)]
            base = jnp.concatenate([e - ev_row for e in energy_j], 1) - ev_col
            for i in range(o):
                wbuf[i] = 1.0 / (eo_col[i:i + 1, :] + base)

        with jax.named_scope("waitR"):
            for group in range(1, len(groups)):
                for rel in range(len(relations)):
                    share(unit, group, rel).wait_recv()
        with jax.named_scope("V"):
            integrals(unit, size * starts[1], total, False)
        with jax.named_scope("waitR0"):
            for rel in range(len(relations)):
                share(unit, 0, rel).wait_recv()
        with jax.named_scope("V0"):
            integrals(unit, 0, size * starts[1], True)

        with jax.named_scope("E"):
            for i in range(0, o, 2):
                x = vbuf[i:i + 2].reshape(2 * v, pair)
                xt = x.T
                turned = pltpu.roll(xt, v, 1)
                top = jnp.where(left, xt[:v], turned[v:])
                bottom = jnp.where(left, turned[:v], xt[v:])
                for k, swap in enumerate((top, bottom)):
                    own_v = x[k * v:(k + 1) * v]
                    ebuf[i + k:i + k + 1, :] = jnp.sum(own_v * (2.0 * own_v - swap) * wbuf[i + k], 0, keepdims=True)
        with jax.named_scope("sum"):
            sums = ebuf[...].T
            return [jnp.sum(sums[h * v:(h + 1) * v], 0, keepdims=True) for h in range(2)]

    pairs = []
    for unit in range(units):
        pairs += energies(unit)
    out_ref[...] = jnp.concatenate(pairs, 0)

    with jax.named_scope("waitS"):
        for unit in range(units):
            for group in range(len(groups)):
                for rel in range(len(relations)):
                    share(unit, group, rel).wait_send()


def solution(mesh):
    size = mesh.shape["dev"]

    def per_device(a_ints, c_occ, c_vir, eps_occ, eps_vir):
        rows, n = a_ints.shape[0], a_ints.shape[1]
        o, v = c_occ.shape[1], c_vir.shape[1]
        units = o // size // 2
        slots = 4
        groups = [g for g in (1, 1, 2, 4) if g < rows]
        while sum(groups) >= rows:
            groups.pop()
        groups.append(rows - sum(groups))
        parts = 4
        dims = (rows, n, o, v, size, slots, units, tuple(groups), parts)
        any_spec = pl.BlockSpec(memory_space=pl.ANY)
        return pl.pallas_call(
            functools.partial(kernel, dims),
            out_shape=pltpu.VMEM((o // size, o), F32),
            in_specs=[any_spec] * 5,
            out_specs=pl.BlockSpec(memory_space=pltpu.VMEM),
            scratch_shapes=[
                pltpu.VMEM((slots, n, n, n), BF16),
                pltpu.VMEM((o, n), BF16),
                pltpu.VMEM((v, n), BF16),
                pltpu.VMEM((1, o), F32),
                pltpu.VMEM((1, v), F32),
                pltpu.VMEM((o, n), BF16),
                pltpu.VMEM((2 * LANES, 2 * v), BF16),
                pltpu.VMEM((o * n, LANES), F32),
                pltpu.VMEM((o // 2 * n, 2 * v), F32),
                pltpu.VMEM((size, units, rows, v, 2 * v), BF16),
                pltpu.VMEM((units, size * rows, v, 2 * v), BF16),
                pltpu.VMEM((o * SUB, size * rows * SUB), BF16),
                pltpu.VMEM((o, v, 2 * v), F32),
                pltpu.VMEM((o, v, 2 * v), F32),
                pltpu.VMEM((o, 2 * v), F32),
                pltpu.SemaphoreType.DMA((slots,)),
                pltpu.SemaphoreType.DMA((parts,)),
                pltpu.SemaphoreType.DMA((4,)),
                pltpu.SemaphoreType.DMA((units, len(groups), size - 1)),
                pltpu.SemaphoreType.DMA((units, len(groups), size - 1)),
            ],
            compiler_params=pltpu.CompilerParams(collective_id=0, has_side_effects=True, vmem_limit_bytes=62 * 2**20),
        )(a_ints, c_occ.T, c_vir.T, eps_occ.reshape(1, o), eps_vir.reshape(1, v)).T

    return jax.shard_map(
        per_device,
        mesh=mesh,
        in_specs=(P(("frag", "dev")), P("frag"), P("frag"), P("frag"), P("frag")),
        out_specs=P("frag", "dev"),
        check_vma=False,
    )
```

time: 157 us -> 48.2 us (0.31)
  waiting for transfers between devices: 76.5 us -> 0 us
  Pallas kernels: 0 us -> 47.5 us
  matrix products: 46 us -> 0 us
  local copies, waits for them, and re-layouts: 22.6 us -> 0.58 us
  starting transfers between devices: 6.85 us -> 0 us
  other arithmetic: 4.9 us -> 0 us
    all_to_all x1 -> x0, waiting for transfers between devices: 76.5 us -> none  [per_device(): half_mo = lax.all_to_all(half_mo, 'dev', 2, 0, tiled=True)]
    pallas_call x0 -> x1, Pallas kernels: none -> 47.5 us  [per_device(): pl.pallas_call(functools.partial(kernel, dims), out_shape=pltpu.VMEM((o /...]
    dot_general x3 -> x0, matrix products: 46 us -> none  [the longest x1 17.7 us: per_device(): jnp.einsum('pjba,pi->jbai', g_mat, c_occ, preferred_element_type=jnp.floa...]
    all_to_all x1 -> x0, local copies, waits for them, and re-layouts: 8.2 us -> none  [per_device(): half_mo = lax.all_to_all(half_mo, 'dev', 2, 0, tiled=True)]
    convert_element_type x1 -> x0, local copies, waits for them, and re-layouts: 7.48 us -> none  [per_device(): jnp.einsum('pqsj,sb->pqjb', t_one, c_vir, preferred_element_type=jnp.floa...]
    all_to_all x1 -> x0, starting transfers between devices: 6.85 us -> none  [per_device(): half_mo = lax.all_to_all(half_mo, 'dev', 2, 0, tiled=True)]
    dot_general x1 -> x0, local copies, waits for them, and re-layouts: 6.78 us -> none  [per_device(): jnp.einsum('pjba,pi->jbai', g_mat, c_occ, preferred_element_type=jnp.floa...]
    reduce_sum x1 -> x0, other arithmetic: 4.75 us -> none  [pair_energies(): pair_ji = jnp.sum(v_mo * (2.0 * v_mo - v_swap) / denominator, axis=(1, 2))]
  transfers between devices with their start and end apart: 1 -> 0, of which waited for: 1 -> 0; matrix products, arithmetic and copies ran while one was open for 0% -> 0% of each run, Pallas kernels for 0% -> 0%
where the time goes in v2:
time: 48.2 us; the launch traced here: 48.1 us
  Pallas kernels  47.5 us (99%)
  local copies, waits for them, and re-layouts  0.58 us (1%)
    pallas_call x1, Pallas kernels, per_device(): pl.pallas_call(functools.partial(kernel, dims), out_shape=pltpu.VMEM((o /...  47.5 us

profile of v2, /device:TPU:81, one launch (start us, length us, event | category | flops | bytes accessed | tf_op | source)
XLA Modules:
  0.0 48.1 jit_solution(15857977577070471893)
XLA Ops:
  0.0 47.5 %shard_map.55 = f32[4,32]{1,0:T(4,128)S(1)} custom-call(bf16[13,104,104,104]{3,2,1,0:T(8,128)(2,1)} %a_hbm.1, bf16[32,104]{1,0:T(8,128)(2,1)} %bitcast.7, bf16[64,104]{1,0:T(8,128)(2,1)} %bitcast.6, f32[1,32]{1,0:T(1,128)} %bitcast.8, f32[1,64]{1,0:T(1,128)} %bitcast.9), custom_call_target="tpu_custom_call" | custom-call | tf_op jit(solution)/shard_map/pallas_call | solution.py:236
  47.5 0.6 %copy.7 = f32[32,4]{0,1:T(4,128)} copy(f32[32,4]{0,1:T(4,128)S(1)} %bitcast.5) | data formatting | bytes 1024

commit v3 on v2

v3 whole, which is shorter than its diff:
```python
import functools

import jax
import jax.numpy as jnp
from jax import lax
from jax.experimental import pallas as pl
from jax.experimental.pallas import tpu as pltpu
from jax.sharding import PartitionSpec as P

MESH = pl.DeviceIdType.MESH
LANES = 128
SUB = 16
F32, BF16 = jnp.float32, jnp.bfloat16


def dot(lhs, rhs):
    return jnp.dot(lhs, rhs, preferred_element_type=F32)


def iota(shape, dim):
    return lax.broadcasted_iota(jnp.int32, shape, dim)


def one_hot(mask):
    return mask.astype(F32).astype(BF16)


def kernel(dims, a_hbm, cot_hbm, cvt_hbm, eo_hbm, ev_hbm, out_ref, abuf, cot, cvt, eo, ev, lhs, wv, tbuf, hbuf, gsend, grecv, kron, vbuf, wbuf, ebuf,
           a_sem, first_sem, c_sem, send_sem, recv_sem):
    rows, n, o, v, size, slots, units, groups, joint, parts = dims
    me, frag = lax.axis_index("dev"), lax.axis_index("frag")
    chips = size // 2
    chip, core = me // 2, me % 2
    pair = 2 * v
    od = o // size
    total = size * rows
    starts = [sum(groups[:g]) for g in range(len(groups))]
    last = len(groups) - 1

    def peer(dx, dc):
        return lax.rem(chip + dx, chips) * 2 + lax.rem(core + dc, 2)

    relations = [(dx, dc) for dx in sorted(range(chips), key=lambda d: -min(d, chips - d)) for dc in range(2) if (dx, dc) != (0, 0)]

    def load(p):
        slot = lax.rem(p, slots)
        return pltpu.make_async_copy(a_hbm.at[p], abuf.at[slot], a_sem.at[slot])

    small = [pltpu.make_async_copy(src, dst, c_sem.at[k]) for k, (src, dst) in enumerate([(cot_hbm, cot), (cvt_hbm, cvt), (eo_hbm, eo), (ev_hbm, ev)])]
    cuts = [0, n * 9 // 16 // 2 * 2, n]
    opening = [pltpu.make_async_copy(a_hbm.at[0, pl.ds(x, y - x)], abuf.at[0, pl.ds(x, y - x)], first_sem.at[k])
               for k, (x, y) in enumerate(zip(cuts, cuts[1:]))]
    small[0].start()
    small[1].start()
    for copy in opening:
        copy.start()
    barrier = pltpu.get_barrier_semaphore()
    for dx, dc in relations:
        pl.semaphore_signal(barrier, inc=1, device_id=(frag, peer(dx, dc)), device_id_type=MESH)

    with jax.named_scope("waitC"):
        small[0].wait()
        small[1].wait()
    for p in range(1, min(slots, rows)):
        load(p).start()
    small[2].start()
    small[3].start()
    row, col = iota((o, o), 0), iota((o, o), 1)
    lhs[...] = dot(one_hot(col == lax.rem(row, size) * od + row // (2 * size) * 2 + lax.rem(row // size, 2)), cot[...]).astype(BF16)
    cv = jnp.pad(cvt[...].astype(F32), ((0, 0), (0, LANES - n))).T.astype(BF16)
    zero = jnp.zeros_like(cv)
    wv[...] = jnp.concatenate([jnp.concatenate([cv, zero], 1), jnp.concatenate([zero, cv], 1)], 0)

    def share(which, group, rel, sem):
        start, count = starts[group], groups[group]
        target = peer(*relations[rel])
        return pltpu.make_async_remote_copy(
            src_ref=gsend.at[target, which, pl.ds(start, count)],
            dst_ref=grecv.at[which, pl.ds(size * start + me * count, count)],
            send_sem=send_sem,
            recv_sem=recv_sem.at[sem],
            device_id=(frag, target),
            device_id_type=MESH,
        )

    def arrivals(which, count, sem):
        part = grecv.at[which, pl.ds(0, (size - 1) * count)]
        return pltpu.make_async_remote_copy(
            src_ref=part, dst_ref=part, send_sem=send_sem, recv_sem=recv_sem.at[sem], device_id=(frag, peer(*relations[0])), device_id_type=MESH)

    every, first_unit, other_units = pl.ds(0, units), pl.ds(0, 1), pl.ds(1, units - 1)

    def send(which, group, sem):
        for rel in range(len(relations)):
            share(which, group, rel, sem).start()

    def occupied(slot, first, end):
        fill = jnp.zeros((n, LANES - n), BF16)
        for q in range(first, end, 2):
            t = dot(lhs[...], jnp.concatenate([abuf[slot, q], fill, abuf[slot, q + 1], fill], 1))
            tbuf[pl.ds(q, o, stride=n), :] = t[:, :LANES]
            tbuf[pl.ds(q + 1, o, stride=n), :] = t[:, LANES:]

    depth = size * n

    def half_mo(unit, first, end):
        even, odd = (tbuf[(2 * unit + k) * depth + first:(2 * unit + k) * depth + end, :] for k in range(2))
        return dot(jnp.concatenate([even, odd], 1).astype(BF16), wv[...])

    def virtual(unit, p):
        with jax.named_scope("step3"):
            for d in range(0, size, 2):
                h = jnp.concatenate([hbuf[unit * depth + k * n:unit * depth + (k + 1) * n, :] for k in (d, d + 1)], 1)
                g = dot(cvt[...], h.astype(BF16)).astype(BF16)
                for k in range(2):
                    gsend[d + k, unit, p] = g[:, k * pair:(k + 1) * pair]

    def open_row():
        for k, copy in enumerate(opening):
            with jax.named_scope("waitA"):
                copy.wait()
            with jax.named_scope("step1"):
                occupied(0, cuts[k], cuts[k + 1])
        if slots < rows:
            load(slots).start()
        for unit in range(units):
            with jax.named_scope("step2"):
                for k in range(2):
                    at = k * depth // 2
                    hbuf[unit * depth + at:unit * depth + at + depth // 2, :] = half_mo(unit, at, at + depth // 2)
            virtual(unit, 0)
            if unit == 0:
                with jax.named_scope("waitB"):
                    pl.semaphore_wait(barrier, len(relations))
            send(pl.ds(unit, 1), 0, 0)

    def next_row(p, carry):
        slot = lax.rem(p, slots)
        with jax.named_scope("waitA"):
            load(p).wait()
        with jax.named_scope("step1"):
            occupied(slot, 0, n)

        @pl.when(p + slots < rows)
        def _():
            load(p + slots).start()

        with jax.named_scope("step2"):
            for unit in range(units):
                hbuf[unit * depth:(unit + 1) * depth, :] = half_mo(unit, 0, depth)
        for unit in range(units):
            virtual(unit, p)
        for group in range(1, len(groups)):
            @pl.when(p == starts[group] + groups[group] - 1)
            def _(group=group):
                if group < joint:
                    send(every, group, 0)
                else:
                    send(first_unit, group, 1)
        return carry

    open_row()
    lax.fori_loop(1, rows, next_row, 0)
    for group in range(joint, len(groups)):
        send(other_units, group, 2 + group - joint)

    small[2].wait()
    small[3].wait()
    with jax.named_scope("kron"):
        by_p = dot(one_hot(iota((o * SUB, o), 0) // SUB == iota((o * SUB, o), 1)), cot[...]).astype(BF16)
        for start, count in zip(starts, groups):
            for at in range(size * start * SUB, size * (start + count) * SUB, 2 * LANES):
                width = min(2 * LANES, size * (start + count) * SUB - at)
                place = (iota((total, width), 1) + at) // SUB - size * start
                spread_p = one_hot(iota((total, width), 0) == place // count * rows + start + place % count)
                same = iota((o * SUB, width), 0) % SUB == iota((o * SUB, width), 1) % SUB
                kron[:, at:at + width] = jnp.where(same, dot(by_p, spread_p), 0.0).astype(BF16)

    for unit in range(units):
        for start, count in zip(starts, groups):
            grecv[unit, pl.ds(size * start + me * count, count)] = gsend[me, unit, start:start + count]

    ev_row, eo_row = ev[...], eo[...]
    diag = iota((v, v), 0) == iota((v, v), 1)
    ev_col = jnp.sum(jnp.where(diag, jnp.broadcast_to(ev_row, (v, v)), 0.0), 1, keepdims=True)
    eo_col = jnp.sum(jnp.where(row == col, jnp.broadcast_to(eo_row, (o, o)), 0.0), 1, keepdims=True)
    left = iota((v, pair), 1) < v

    def weights(unit):
        with jax.named_scope("W"):
            energy_j = [jnp.sum(jnp.where(iota((1, o), 1) == me * od + 2 * unit + h, eo_row, 0.0), 1, keepdims=True) for h in range(2)]
            base = jnp.concatenate([e - ev_row for e in energy_j], 1) - ev_col
            for i in range(o):
                wbuf[i] = 1.0 / (eo_col[i:i + 1, :] + base)

    def integrals(unit, first, end, add):
        with jax.named_scope("V"):
            width = (end - first) * SUB
            for block in range(0, v, 2 * SUB):
                rhs = jnp.concatenate([grecv[unit, first:end, block + k * SUB:block + (k + 1) * SUB, :].reshape(width, pair) for k in range(2)], 1)
                part = dot(kron[:, first * SUB:end * SUB], rhs)
                for k in range(2):
                    at = slice(block + k * SUB, block + (k + 1) * SUB)
                    new = part[:, k * pair:(k + 1) * pair].reshape(o, SUB, pair)
                    vbuf[:, at, :] = vbuf[:, at, :] + new if add else new

    def energies():
        with jax.named_scope("E"):
            for i in range(0, o, 2):
                x = vbuf[i:i + 2].reshape(2 * v, pair)
                xt = x.T
                turned = pltpu.roll(xt, v, 1)
                top = jnp.where(left, xt[:v], turned[v:])
                bottom = jnp.where(left, turned[:v], xt[v:])
                for k, swap in enumerate((top, bottom)):
                    own = x[k * v:(k + 1) * v]
                    ebuf[i + k:i + k + 1, :] = jnp.sum(own * (2.0 * own - swap) * wbuf[i + k], 0, keepdims=True)

    def totals():
        with jax.named_scope("sum"):
            sums = ebuf[...].T
            return [jnp.sum(sums[h * v:(h + 1) * v], 0, keepdims=True) for h in range(2)]

    pairs = []
    for unit in range(units):
        weights(unit)
        if unit == 0:
            with jax.named_scope("waitR"):
                arrivals(every, starts[joint], 0).wait_recv()
                arrivals(first_unit, rows - starts[joint], 1).wait_recv()
            integrals(unit, 0, total, False)
        else:
            for group in range(joint, len(groups)):
                if unit == 1:
                    with jax.named_scope(f"waitR{group}"):
                        arrivals(other_units, groups[group], 2 + group - joint).wait_recv()
                first = group == joint
                integrals(unit, 0 if first else size * starts[group], size * (starts[group] + groups[group]), not first)
        energies()
        pairs += totals()
    out_ref[...] = jnp.concatenate(pairs, 0)

    sent = gsend.at[pl.ds(0, size - 1)]
    with jax.named_scope("waitS"):
        pltpu.make_async_remote_copy(
            src_ref=sent, dst_ref=sent, send_sem=send_sem, recv_sem=recv_sem.at[0], device_id=(frag, peer(*relations[0])), device_id_type=MESH).wait_send()


def solution(mesh):
    size = mesh.shape["dev"]

    def per_device(a_ints, c_occ, c_vir, eps_occ, eps_vir):
        rows, n = a_ints.shape[0], a_ints.shape[1]
        o, v = c_occ.shape[1], c_vir.shape[1]
        units = o // size // 2
        slots, parts = 4, 2
        groups = (1, 1, 2, rows - 8, 2, 2)
        joint = 3
        dims = (rows, n, o, v, size, slots, units, groups, joint, parts)
        any_spec = pl.BlockSpec(memory_space=pl.ANY)
        return pl.pallas_call(
            functools.partial(kernel, dims),
            out_shape=pltpu.VMEM((o // size, o), F32),
            in_specs=[any_spec] * 5,
            out_specs=pl.BlockSpec(memory_space=pltpu.VMEM),
            scratch_shapes=[
                pltpu.VMEM((slots, n, n, n), BF16),
                pltpu.VMEM((o, n), BF16),
                pltpu.VMEM((v, n), BF16),
                pltpu.VMEM((1, o), F32),
                pltpu.VMEM((1, v), F32),
                pltpu.VMEM((o, n), BF16),
                pltpu.VMEM((2 * LANES, 2 * v), BF16),
                pltpu.VMEM((o * n, LANES), F32),
                pltpu.VMEM((units * size * n, 2 * v), F32),
                pltpu.VMEM((size, units, rows, v, 2 * v), BF16),
                pltpu.VMEM((units, size * rows, v, 2 * v), BF16),
                pltpu.VMEM((o * SUB, size * rows * SUB), BF16),
                pltpu.VMEM((o, v, 2 * v), F32),
                pltpu.VMEM((o, v, 2 * v), F32),
                pltpu.VMEM((o, 2 * v), F32),
                pltpu.SemaphoreType.DMA((slots,)),
                pltpu.SemaphoreType.DMA((parts,)),
                pltpu.SemaphoreType.DMA((4,)),
                pltpu.SemaphoreType.DMA,
                pltpu.SemaphoreType.DMA((2 + len(groups) - joint,)),
            ],
            compiler_params=pltpu.CompilerParams(collective_id=0, has_side_effects=True, vmem_limit_bytes=62 * 2**20),
        )(a_ints, c_occ.T, c_vir.T, eps_occ.reshape(1, o), eps_vir.reshape(1, v)).T

    return jax.shard_map(
        per_device,
        mesh=mesh,
        in_specs=(P(("frag", "dev")), P("frag"), P("frag"), P("frag"), P("frag")),
        out_specs=P("frag", "dev"),
        check_vma=False,
    )
```

time: 48.2 us -> 45.5 us (0.944)
  Pallas kernels: 47.5 us -> 44.8 us
    pallas_call x1, Pallas kernels: 47.5 us -> 44.8 us  [per_device(): pl.pallas_call(functools.partial(kernel, dims), out_shape=pltpu.VMEM((o /...]
where the time goes in v3:
time: 45.5 us; the launch traced here: 45.4 us
  Pallas kernels  44.8 us (98%)
  local copies, waits for them, and re-layouts  0.58 us (1%)
    pallas_call x1, Pallas kernels, per_device(): pl.pallas_call(functools.partial(kernel, dims), out_shape=pltpu.VMEM((o /...  44.8 us

profile of v3, /device:TPU:81, one launch (start us, length us, event | category | flops | bytes accessed | tf_op | source)
XLA Modules:
  0.0 45.4 jit_solution(988263887497828669)
XLA Ops:
  0.0 44.8 %shard_map.55 = f32[4,32]{1,0:T(4,128)S(1)} custom-call(bf16[13,104,104,104]{3,2,1,0:T(8,128)(2,1)} %a_hbm.1, bf16[32,104]{1,0:T(8,128)(2,1)} %bitcast.7, bf16[64,104]{1,0:T(8,128)(2,1)} %bitcast.6, f32[1,32]{1,0:T(1,128)} %bitcast.8, f32[1,64]{1,0:T(1,128)} %bitcast.9), custom_call_target="tpu_custom_call" | custom-call | tf_op jit(solution)/shard_map/pallas_call | solution.py:261
  44.8 0.6 %copy.7 = f32[32,4]{0,1:T(4,128)} copy(f32[32,4]{0,1:T(4,128)S(1)} %bitcast.5) | data formatting | bytes 1024

commit v4 on v3

--- a/solution.py
+++ b/solution.py
@@ -209,9 +209,9 @@
             for i in range(0, o, 2):
                 x = vbuf[i:i + 2].reshape(2 * v, pair)
                 xt = x.T
-                turned = pltpu.roll(xt, v, 1)
-                top = jnp.where(left, xt[:v], turned[v:])
-                bottom = jnp.where(left, turned[:v], xt[v:])
+                turned = pltpu.roll(jnp.where(left, xt[v:], xt[:v]), v, 1)
+                top = jnp.where(left, xt[:v], turned)
+                bottom = jnp.where(left, turned, xt[v:])
                 for k, swap in enumerate((top, bottom)):
                     own = x[k * v:(k + 1) * v]
                     ebuf[i + k:i + k + 1, :] = jnp.sum(own * (2.0 * own - swap) * wbuf[i + k], 0, keepdims=True)

time: 45.5 us -> 45.4 us (level)
  no operation moved by 1% of the time
where the time goes in v4:
time: 45.4 us; the launch traced here: 45.3 us
  Pallas kernels  44.7 us (98%)
  local copies, waits for them, and re-layouts  0.58 us (1%)
    pallas_call x1, Pallas kernels, per_device(): pl.pallas_call(functools.partial(kernel, dims), out_shape=pltpu.VMEM((o /...  44.7 us

profile of v4, /device:TPU:81, one launch (start us, length us, event | category | flops | bytes accessed | tf_op | source)
XLA Modules:
  0.0 45.3 jit_solution(11794871138484969944)
XLA Ops:
  0.0 44.7 %shard_map.55 = f32[4,32]{1,0:T(4,128)S(1)} custom-call(bf16[13,104,104,104]{3,2,1,0:T(8,128)(2,1)} %a_hbm.1, bf16[32,104]{1,0:T(8,128)(2,1)} %bitcast.7, bf16[64,104]{1,0:T(8,128)(2,1)} %bitcast.6, f32[1,32]{1,0:T(1,128)} %bitcast.8, f32[1,64]{1,0:T(1,128)} %bitcast.9), custom_call_target="tpu_custom_call" | custom-call | tf_op jit(solution)/shard_map/pallas_call | solution.py:261
  44.7 0.6 %copy.7 = f32[32,4]{0,1:T(4,128)} copy(f32[32,4]{0,1:T(4,128)S(1)} %bitcast.5) | data formatting | bytes 1024

commit v5 on v4

--- a/solution.py
+++ b/solution.py
@@ -255,7 +255,7 @@
         units = o // size // 2
         slots, parts = 4, 2
         groups = (1, 1, 2, rows - 8, 2, 2)
-        joint = 3
+        joint = 4
         dims = (rows, n, o, v, size, slots, units, groups, joint, parts)
         any_spec = pl.BlockSpec(memory_space=pl.ANY)
         return pl.pallas_call(

time: 45.4 us -> 45.4 us (level)
  no operation moved by 1% of the time
where the time goes in v5:
time: 45.4 us; the launch traced here: 45.3 us
  Pallas kernels  44.7 us (98%)
  local copies, waits for them, and re-layouts  0.58 us (1%)
    pallas_call x1, Pallas kernels, per_device(): pl.pallas_call(functools.partial(kernel, dims), out_shape=pltpu.VMEM((o /...  44.7 us

profile of v5, /device:TPU:81, one launch (start us, length us, event | category | flops | bytes accessed | tf_op | source)
XLA Modules:
  0.0 45.3 jit_solution(10497047742588850619)
XLA Ops:
  0.0 44.7 %shard_map.55 = f32[4,32]{1,0:T(4,128)S(1)} custom-call(bf16[13,104,104,104]{3,2,1,0:T(8,128)(2,1)} %a_hbm.1, bf16[32,104]{1,0:T(8,128)(2,1)} %bitcast.7, bf16[64,104]{1,0:T(8,128)(2,1)} %bitcast.6, f32[1,32]{1,0:T(1,128)} %bitcast.8, f32[1,64]{1,0:T(1,128)} %bitcast.9), custom_call_target="tpu_custom_call" | custom-call | tf_op jit(solution)/shard_map/pallas_call | solution.py:261
  44.7 0.6 %copy.7 = f32[32,4]{0,1:T(4,128)} copy(f32[32,4]{0,1:T(4,128)S(1)} %bitcast.5) | data formatting | bytes 1024
